TPU v7x, 32 devices: a whole 2x2x4 slice. The times are simulated.
32 devices in a mesh: dp: 8 (over z, x), cand: 4 (over y, core).
Axes of the slice: x: 2, y: 2, z: 4, core: 2. Of those that a mesh axis runs over, the one named last changes fastest.
Arguments:
- hidden: bfloat16 [16, 32, 128, 768], P('dp', 'cand'), may hold values from -24 to 24
- attn_weight: bfloat16 [768, 3072], P('dp'), may hold values from -1 to 1
- norm_gain: float32 [768], replicated, may hold values from 0.2 to 4
- pos_bias: float32 [12, 128, 128], replicated, may hold values from -5 to 5
- score_weight: float32 [768], replicated, may hold values from -4 to 4
- pair_lengths: int32 [16, 32], P('dp', 'cand'), may hold values from 32 to 128
- labels: int32 [16, 32], P('dp', 'cand'), may hold values from 0 to 3
Outputs:
- update: float32 [768, 3072], P('dp')
- loss: float32 [16], P('dp')
All inputs are finite; a program needn't handle non-finite values.
Results may differ from a plain program's by a relative error of at most 0.017.
Values may be sent and summed in bfloat16 or wider, within the bound.
No kernel may reach another device: no remote copies, remote signals or barrier semaphores. Data moves between devices by JAX's collectives and lax.ppermute only.
A program may use at most 128 MiB of HBM per device.

v0:
```python
import jax
import jax.numpy as jnp
from jax import lax
from jax.sharding import PartitionSpec as P

EPS = 1e-06


def rms_rows(values, gain):
    factor = lax.rsqrt(jnp.mean(values * values, axis=-1, keepdims=True) + EPS)
    return values * factor * gain


def attend(qkv, pos_bias, pair_len):
    batch, seq, triple = qkv.shape
    width = triple // 3
    heads = pos_bias.shape[0]
    head_size = width // heads
    parts = qkv.reshape(batch, seq, 3, heads, head_size)
    logits = jnp.einsum(
        "bqhd,bkhd->bhqk", parts[:, :, 0], parts[:, :, 1], preferred_element_type=jnp.float32
    )
    logits = logits + pos_bias[None]
    valid = jnp.arange(seq, dtype=jnp.int32)[None, :] < pair_len[:, None]
    logits = jnp.where(valid[:, None, None, :], logits, -1e30)
    highest = jnp.max(logits, axis=-1, keepdims=True)
    expo = jnp.exp(logits - highest)
    probs = (expo / jnp.sum(expo, axis=-1, keepdims=True)).astype(jnp.bfloat16)
    context = jnp.einsum(
        "bhqk,bkhd->bqhd", probs, parts[:, :, 2], preferred_element_type=jnp.float32
    )
    return context.astype(jnp.bfloat16).reshape(batch, seq, width)


def score_head(pooled, score_weight):
    return jnp.sum(rms_rows(pooled, 1.0) * score_weight, axis=-1)


def shards(hidden, attn_weight, norm_gain, pos_bias, score_weight, pair_lengths, labels):
    q_local, c_local, seq, width = hidden.shape
    weights = lax.all_gather(attn_weight, "dp", axis=0, tiled=True)
    tokens = hidden.reshape(q_local * c_local, seq, width)
    pair_len = pair_lengths.reshape(-1)
    values = tokens.astype(jnp.float32)
    normed = rms_rows(values, norm_gain).astype(jnp.bfloat16)
    flat_norm = normed.reshape(-1, width)
    qkv = jnp.dot(flat_norm, weights[:, : 3 * width], preferred_element_type=jnp.float32)
    qkv = qkv.astype(jnp.bfloat16).reshape(q_local * c_local, seq, 3 * width)
    context, attend_back = jax.vjp(lambda block: attend(block, pos_bias, pair_len), qkv)
    flat_ctx = context.reshape(-1, width)
    out_rows = values + jnp.dot(
        flat_ctx, weights[:, 3 * width :], preferred_element_type=jnp.float32
    ).reshape(values.shape)
    live = (jnp.arange(seq, dtype=jnp.int32)[None, :] < pair_len[:, None]).astype(jnp.float32)
    share = live / pair_len.astype(jnp.float32)[:, None]
    pooled = jnp.sum(out_rows * share[:, :, None], axis=1)
    flat_scores, head_back = jax.vjp(lambda vector: score_head(vector, score_weight), pooled)
    scores = flat_scores.reshape(q_local, c_local)
    target = jnp.exp(labels.astype(jnp.float32))
    highest = lax.pmax(jnp.max(scores, axis=1), "cand")
    expsum, target_sum, target_dot = lax.psum(
        (
            jnp.sum(jnp.exp(scores - highest[:, None]), axis=1),
            jnp.sum(target, axis=1),
            jnp.sum(target * scores, axis=1),
        ),
        "cand",
    )
    loss = highest + jnp.log(expsum) - target_dot / target_sum
    score_grad = jnp.exp(scores - highest[:, None]) / expsum[:, None] - target / target_sum[:, None]
    pooled_grad = head_back(score_grad.reshape(-1))[0]
    out_grad = (pooled_grad[:, None, :] * share[:, :, None]).astype(jnp.bfloat16)
    flat_out = out_grad.reshape(-1, width)
    context_grad = jnp.dot(flat_out, weights[:, 3 * width :].T, preferred_element_type=jnp.float32)
    context_grad = context_grad.astype(jnp.bfloat16).reshape(context.shape)
    qkv_grad = attend_back(context_grad)[0].reshape(-1, 3 * width)
    dims = (((0,), (0,)), ((), ()))
    first = lax.dot_general(flat_norm, qkv_grad, dims, preferred_element_type=jnp.float32)
    second = lax.dot_general(flat_ctx, flat_out, dims, preferred_element_type=jnp.float32)
    shard = lax.psum_scatter(
        jnp.concatenate([first, second], axis=1).astype(jnp.bfloat16),
        "dp",
        scatter_dimension=0,
        tiled=True,
    ).astype(jnp.float32)
    shard = lax.psum(shard.astype(jnp.bfloat16), "cand").astype(jnp.float32)
    squares = lax.psum(jnp.sum(shard * shard), "dp")
    rms_value = jnp.sqrt(squares / (4.0 * width * width))
    update = shard / (rms_value + EPS)
    return (update, loss)


def solution(mesh):
    in_specs = (
        P("dp", "cand", None, None),
        P("dp", None),
        P(),
        P(),
        P(),
        P("dp", "cand"),
        P("dp", "cand"),
    )
    out_specs = (P("dp", None), P("dp"))
    return jax.shard_map(shards, mesh=mesh, in_specs=in_specs, out_specs=out_specs, check_vma=False)
```

profile of v0, /device:TPU:0, one launch (start us, length us, event | category | flops | bytes accessed | tf_op | source)
XLA Modules:
  0.0 460.7 jit_solution(10536083495842605806)
XLA Ops:
  7.2 0.0 copy-start.5
  7.2 0.0 all-gather.2.cloned.1.call-start
  7.2 0.7 all-gather.2.cloned.1.call-update
  7.9 0.0 reduce-scatter.2.cloned.1.call-start
  8.0 0.9 lt.33
  8.9 2.3 copy.24
  11.2 0.1 iota_compare_fusion
  11.2 0.1 fusion.51
  11.3 2.6 multiply_reduce_fusion
  13.9 2.5 multiply_convert_fusion.1
  16.4 2.4 fusion.13
  18.8 73.4 %all-gather.2.cloned.1.call-done = bf16[768,3072]{1,0:T(8,128)(2,1)} async-done(((bf16[96,3072]{1,0:T(8,128)(2,1)}), bf16[768,3072]{1,0:T(8,128)(2,1)}) %all-gather.2.cloned.1.call-update) | async-done | bytes 4718608 | tf_op jit(solution)/shard_map/all_gather | solution.py:41
  92.3 12.5 %convolution_convert_fusion = bf16[2048,2304]{1,0:T(8,128)(2,1)} fusion(bf16[2048,768]{1,0:T(8,128)(2,1)} %fusion.13, bf16[768,3072]{1,0:T(8,128)(2,1)} %all-gather.2.cloned.1.call-done), kind=kOutput, calls=%fused_computation.11 | convolution fusion | flops 7252475904 | bytes 16121856 | tf_op jit(solution)/shard_map/dot_general | solution.py:47
  104.8 12.7 %copy.20 = bf16[2048,2304]{0,1:T(8,128)(2,1)} copy(bf16[2048,2304]{1,0:T(8,128)(2,1)} %convolution_convert_fusion) | data formatting | bytes 18874368 | tf_op jit(solution)/shard_map/convert_element_type | solution.py:48
  117.5 10.9 %copy.45 = bf16[288,8,16,128]{3,2,1,0:T(8,128)(2,1)} copy(bf16[288,8,16,128]{3,1,2,0:T(8,128)(2,1)} %bitcast.104) | data formatting | bytes 18874368
  128.4 6.4 %fusion.56 = (bf16[16,128,1,12,64]{1,0,4,3,2:T(8,128)(2,1)}, bf16[16,128,1,12,64]{1,0,4,3,2:T(8,128)(2,1)}, bf16[16,128,1,12,64]{1,0,4,3,2:T(8,128)(2,1)S(1)}) fusion(bf16[16,128,3,12,64]{1,0,4,3,2:T(8,128)(2,1)} %bitcast.103), kind=kLoop, calls=%fused_computation.91 | loop fusion | bytes 18874368 | tf_op jit(solution)/shard_map/jvp()/slice | solution.py:30
  134.8 7.5 %fusion.5 = (f32[16,12,128]{2,1,0:T(8,128)S(1)}, f32[16,12,128,128]{2,3,1,0:T(8,128)S(1)}) fusion(f32[12,128,128]{1,2,0:T(8,128)S(1)} %copy-done.11, pred[16,128]{1,0:T(8,128)(4,1)S(1)} %iota_compare_fusion, bf16[16,128,1,12,64]{1,0,4,3,2:T(8,128)(2,1)S(1)} %get-tuple-element.15, bf16[16,128,1,12,64]{1,0,4,3,2:T(8,128)(2,1)} %get-tuple-element.14), kind=kOutput, calls=%fused_computation.13 | convolution fusion | flops 412065792 | bytes 19761152 | tf_op jit(solution)/shard_map/jvp(bqhd,bkhd->bhqk)/dot_general | solution.py:20
  142.3 3.4 fusion.37
  145.7 1.2 copy-done
  146.9 8.1 %convert_reduce_fusion = (f32[16,12,128]{2,1,0:T(8,128)S(1)}, pred[16,12,128,128]{2,3,1,0:T(32,128)(4,1)}, bf16[16,12,128,128]{2,3,1,0:T(8,128)(2,1)S(1)}) fusion(f32[16,12,128]{2,1,0:T(8,128)S(1)} %get-tuple-element.20, f32[16,12,128,128]{2,3,1,0:T(8,128)S(1)} %get-tuple-element.21, f32[12,128,128]{1,2,0:T(8,128)S(1)} %copy-done.11, ...), kind=kLoop, calls=%fused_computation.7 | loop fusion | flops 25141248 | bytes 23103488 | tf_op jit(solution)/shard_map/jvp()/reduce_sum | solution.py:26
  155.0 2.7 fusion.36
  157.7 0.4 copy-done.2
  158.2 1.0 copy-done.6
  159.2 4.6 fusion.15
  163.8 0.1 multiply_reduce_fusion.2
  163.9 0.2 multiply_reduce_fusion.1
  164.1 0.1 reshape.246
  164.2 0.1 reduce_max.19
  164.3 5.7 %pmax.7 = f32[2]{0:T(128)S(1)} all-reduce(f32[2]{0:T(128)S(1)} %reduce_max.19), channel_id=1, replica_groups=mesh['dp'=8,'cand'=4] {'cand'}, use_global_device_ids=true, to_apply=%region_7.8 | all-reduce | flops 2 | bytes 16 | tf_op jit(solution)/shard_map/pmax | solution.py:60
  170.0 0.2 multiply_reduce_fusion.3
  170.2 6.6 %all-reduce.3 = (f32[2]{0:T(128)S(1)}, f32[2]{0:T(128)S(1)}, f32[2]{0:T(128)S(1)}) all-reduce(f32[2]{0:T(128)S(1)} %get-tuple-element.3, f32[2]{0:T(128)S(1)} %get-tuple-element.4, f32[2]{0:T(128)S(1)} %get-tuple-element.2), channel_id=1, replica_groups=mesh['dp'=8,'cand'=4] {'cand'}, use_global_device_ids=true, to_apply=%region_11.12 | all-reduce | flops 6 | bytes 48 | tf_op jit(solution)/shard_map/psum | solution.py:61
  176.8 0.1 divide_subtract_fusion
  176.9 0.1 broadcast_in_dim.34
  177.0 0.2 fusion.45
  177.2 0.1 add_add_fusion
  177.3 0.4 fusion.11
  177.7 5.3 %convolution_convert_fusion.2 = bf16[2048,768]{1,0:T(8,128)(2,1)} fusion(bf16[2048,768]{1,0:T(8,128)(2,1)S(1)} %fusion.11, bf16[768,3072]{1,0:T(8,128)(2,1)} %all-gather.2.cloned.1.call-done), kind=kOutput, calls=%fused_computation.41 | convolution fusion | flops 2417491968 | bytes 7471104 | tf_op jit(solution)/shard_map/dot_general | solution.py:74
  182.9 4.7 %copy.27 = bf16[2048,768]{0,1:T(8,128)(2,1)} copy(bf16[2048,768]{1,0:T(8,128)(2,1)} %convolution_convert_fusion.2) | data formatting | bytes 6291456 | tf_op jit(solution)/shard_map/convert_element_type | solution.py:75
  187.7 2.9 copy.46
  190.6 1.6 copy-done.13
  192.2 9.0 %convert_bitcast_fusion.2 = bf16[16,128,1,12,64]{1,4,3,0,2:T(8,128)(2,1)} fusion(bf16[16,12,128,128]{2,3,1,0:T(8,128)(2,1)} %copy-done.2, bf16[16,12,64,128]{3,0,2,1:T(8,128)(2,1)S(1)} %bitcast.108), kind=kOutput, calls=%fused_computation.50 | convolution fusion | flops 404226048 | bytes 12582912 | tf_op jit(solution)/shard_map/transpose(jvp(bhqk,bkhd->bqhd))/dot_general | solution.py:29
  201.2 12.6 %fusion.3 = (f32[16,12,128]{2,1,0:T(8,128)S(1)}, bf16[16,12,128,128]{2,3,1,0:T(8,128)(2,1)}) fusion(f32[16,12,128]{2,1,0:T(8,128)S(1)} %multiply_divide_fusion, f32[16,12,128]{2,1,0:T(8,128)S(1)} %get-tuple-element.20, f32[16,12,128,128]{2,3,1,0:T(8,128)} %copy-done, f32[12,128,128]{1,2,0:T(8,128)S(1)} %copy-done.11, ...), kind=kOutput, calls=%fused_computation.5 | convolution fusion | flops 427794432 | bytes 26249216 | tf_op jit(solution)/shard_map/transpose(jvp(bhqk,bkhd->bqhd))/dot_general | solution.py:29
  213.9 10.1 %fusion.53 = (f32[16,12,128]{2,1,0:T(8,128)S(1)}, f32[16,12,128,128]{2,3,1,0:T(8,128)}) fusion(f32[16,12,128]{2,1,0:T(8,128)S(1)} %get-tuple-element.20, f32[16,12,128,128]{2,3,1,0:T(8,128)S(1)} %bitcast.102, f32[12,128,128]{1,2,0:T(8,128)S(1)} %copy-done.11, pred[16,128]{1,0:T(8,128)(4,1)S(1)} %iota_compare_fusion, f32[16,12,128]{2,1,0:T(8,128)S(1)} %neg.9, ...), kind=kLoop, calls=%fused_computation.90 | loop fusion | flops 25141248 | bytes 32638976 | tf_op jit(solution)/shard_map/transpose(jvp())/reduce_sum | solution.py:27
  224.1 11.4 %convert_bitcast_fusion.1 = bf16[16,128,1,12,64]{1,4,3,0,2:T(8,128)(2,1)} fusion(bf16[16,128,1,12,64]{1,0,4,3,2:T(8,128)(2,1)} %get-tuple-element.14, f32[16,12,128,128]{2,3,1,0:T(8,128)} %get-tuple-element.9, pred[16,12,128,128]{2,3,1,0:T(32,128)(4,1)} %get-tuple-element.11, f32[16,12,128]{2,1,0:T(8,128)S(1)} %negate_divide_fusion, ...), kind=kOutput, calls=%fused_computation.49 | convolution fusion | flops 413663232 | bytes 22120448 | tf_op jit(solution)/shard_map/transpose(jvp(bqhd,bkhd->bhqk))/dot_general | solution.py:20
  235.5 0.5 copy-done.4
  235.9 1.0 copy-done.7
  237.0 4.2 convert_bitcast_fusion
  241.2 2.1 multiply_convert_fusion
  243.3 0.9 copy-done.12
  244.2 6.8 %pad_add_fusion = bf16[16,128,3,12,64]{1,4,3,0,2:T(8,128)(2,1)} fusion(bf16[16,128,1,12,64]{1,4,3,0,2:T(8,128)(2,1)} %convert_bitcast_fusion, bf16[16,128,1,12,64]{1,4,3,0,2:T(8,128)(2,1)} %convert_bitcast_fusion.1, bf16[16,128,1,12,64]{1,4,3,0,2:T(8,128)(2,1)S(1)} %copy-done.12), kind=kLoop, calls=%fused_computation.17 | loop fusion | flops 9437184 | bytes 18874368 | tf_op jit(solution)/shard_map/transpose(jvp())/add_any | solution.py:21
  251.0 26.1 %copy.33 = bf16[16,128,3,12,64]{1,0,4,3,2:T(8,128)(2,1)} copy(bf16[16,128,3,12,64]{1,4,3,0,2:T(8,128)(2,1)} %pad_add_fusion) | data formatting | bytes 18874368 | tf_op jit(solution)/shard_map/transpose(jvp())/add_any | solution.py:21
  277.2 2.4 copy.34
  279.6 11.4 %fusion.22 = bf16[768,2304]{1,0:T(8,128)(2,1)S(1)} fusion(bf16[2048,768]{1,0:T(8,128)(2,1)S(1)} %bitcast.113, bf16[288,8,16,128]{3,2,1,0:T(8,128)(2,1)} %bitcast.110), kind=kOutput, calls=%fused_computation.37 | convolution fusion | flops 7249526784 | bytes 16121856 | tf_op jit(solution)/shard_map/dot_general | solution.py:78
  291.0 2.6 fusion.38
  293.7 2.8 pad_maximum_fusion
  296.4 0.0 reduce-scatter.2.cloned.1.call-update
  296.5 0.0 all-reduce.6.cloned.1.call-start
  296.5 94.1 %reduce-scatter.2.cloned.1.call-done = bf16[96,3072]{1,0:T(8,128)(2,1)} async-done(((bf16[768,3072]{1,0:T(8,128)(2,1)}), bf16[96,3072]{1,0:T(8,128)(2,1)}) %reduce-scatter.2.cloned.1.call-update) | async-done | bytes 589840 | tf_op jit(solution)/shard_map/reduce_scatter | solution.py:80
  390.6 0.0 all-reduce.6.cloned.1.call-update
  390.6 35.8 %all-reduce.6.cloned.1.call-done = bf16[96,3072]{1,0:T(8,128)(2,1)} async-done(((bf16[96,3072]{1,0:T(8,128)(2,1)}), bf16[96,3072]{1,0:T(8,128)(2,1)}) %all-reduce.6.cloned.1.call-update) | async-done | bytes 589840 | tf_op jit(solution)/shard_map/psum | solution.py:86
  426.4 2.0 fusion.41
  428.4 0.5 divide_subtract_fusion.1
  428.9 22.0 %psum.38 = f32[]{:T(128)} all-reduce(f32[]{:T(128)} %fusion.41), channel_id=1, replica_groups=mesh['dp'=8,'cand'=4] {'dp'}, use_global_device_ids=true, to_apply=%region_19.20 | all-reduce | flops 1 | bytes 8 | tf_op jit(solution)/shard_map/psum | solution.py:87
  451.6 2.2 convert_divide_fusion.1
  (44 shorter events, 0.2 us)
Async XLA Ops:
  7.2 6.8 %copy-start.5 = (bf16[2,8,128,768]{3,2,1,0:T(8,128)(2,1)S(1)}, bf16[2,8,128,768]{3,2,1,0:T(8,128)(2,1)}, u32[]{:S(2)}) copy-start(bf16[2,8,128,768]{3,2,1,0:T(8,128)(2,1)} %param.7) | copy-start | bytes 9437188
  7.2 6.8 %copy-start.17 = (f32[768]{0:T(1024)S(1)}, f32[768]{0:T(1024)}, u32[]{:S(2)}) copy-start(f32[768]{0:T(1024)} %param.9) | copy-start | bytes 9220
  7.2 85.1 %all-gather.2.cloned.1.call-start = ((), (), s32[]{:S(2)}) async-start(), calls=%async_computation.1 | async-start | bytes 5308416 | tf_op jit(solution)/shard_map/all_gather | solution.py:41
  7.9 382.7 %reduce-scatter.2.cloned.1.call-start = ((), (), s32[]{:S(2)}) async-start(), calls=%async_computation.2 | async-start | bytes 5308416 | tf_op jit(solution)/shard_map/reduce_scatter | solution.py:80
  128.4 6.4 %copy-start.11 = (f32[12,128,128]{1,2,0:T(8,128)S(1)}, f32[12,128,128]{1,2,0:T(8,128)}, u32[]{:S(2)}) copy-start(f32[12,128,128]{1,2,0:T(8,128)} %copy.24) | copy-start | bytes 2359300
  134.8 7.6 %copy-start.3 = (bf16[16,128,1,12,64]{1,0,4,3,2:T(8,128)(2,1)}, bf16[16,128,1,12,64]{1,0,4,3,2:T(8,128)(2,1)S(1)}, u32[]{:S(2)}) copy-start(bf16[16,128,1,12,64]{1,0,4,3,2:T(8,128)(2,1)S(1)} %get-tuple-element.15) | copy-start | bytes 9437188
  142.3 4.6 copy-start
  146.9 8.1 %copy-start.8 = (bf16[16,128,1,12,64]{1,0,4,3,2:T(8,128)(2,1)S(1)}, bf16[16,128,1,12,64]{1,0,4,3,2:T(8,128)(2,1)}, u32[]{:S(2)}) copy-start(bf16[16,128,1,12,64]{1,0,4,3,2:T(8,128)(2,1)} %get-tuple-element.13) | copy-start | bytes 9437188
  155.0 3.2 copy-start.2
  155.0 4.2 copy-start.6
  158.2 5.6 %copy-start.9 = (bf16[16,12,64,128]{3,2,1,0:T(8,128)(2,1)}, bf16[16,12,64,128]{3,2,1,0:T(8,128)(2,1)S(1)}, u32[]{:S(2)}) copy-start(bf16[16,12,64,128]{3,2,1,0:T(8,128)(2,1)S(1)} %fusion.36) | copy-start | bytes 9437188
  159.2 4.7 %copy-start.16 = (f32[768]{0:T(1024)S(1)}, f32[768]{0:T(1024)}, u32[]{:S(2)}) copy-start(f32[768]{0:T(1024)} %param.11) | copy-start | bytes 9220
  159.2 10.8 %copy-start.18 = (s32[2,8]{1,0:T(2,128)S(1)}, s32[2,8]{1,0:T(2,128)}, u32[]{:S(2)}) copy-start(s32[2,8]{1,0:T(2,128)} %param.13) | copy-start | bytes 196
  190.5 1.6 copy-start.13
  192.2 21.7 %slice-start = ((s8[12582912]{0:T(1024)(128)(4,1)}), s8[4194304]{0:T(1024)(128)(4,1)S(1)}, s32[]{:S(2)}) async-start(s8[12582912]{0:T(1024)(128)(4,1)} %bitcast.101), calls=%async_computation.4 | async-start | bytes 8388608
  201.2 12.7 %slice-start.1 = ((s8[12582912]{0:T(1024)(128)(4,1)}), s8[4194304]{0:T(1024)(128)(4,1)S(1)}, s32[]{:S(2)}) async-start(s8[12582912]{0:T(1024)(128)(4,1)} %bitcast.101), calls=%async_computation.5 | async-start | bytes 8388608
  201.2 12.7 %slice-start.2 = ((s8[12582912]{0:T(1024)(128)(4,1)}), s8[4194304]{0:T(1024)(128)(4,1)S(1)}, s32[]{:S(2)}) async-start(s8[12582912]{0:T(1024)(128)(4,1)} %bitcast.101), calls=%async_computation.6 | async-start | bytes 8388608
  224.1 11.4 %copy-start.1 = (f32[16,12,128,128]{2,3,1,0:T(8,128)S(1)}, f32[16,12,128,128]{2,3,1,0:T(8,128)}, u32[]{:S(2)}) copy-start(f32[16,12,128,128]{2,3,1,0:T(8,128)} %get-tuple-element.9) | copy-start | bytes 37748740
  224.1 11.8 %copy-start.4 = (bf16[16,128,1,12,64]{1,0,4,3,2:T(8,128)(2,1)S(1)}, bf16[16,128,1,12,64]{1,0,4,3,2:T(8,128)(2,1)}, u32[]{:S(2)}) copy-start(bf16[16,128,1,12,64]{1,0,4,3,2:T(8,128)(2,1)} %copy-done.3) | copy-start | bytes 9437188
  224.1 12.9 %copy-start.7 = (pred[16,12,128,128]{2,3,1,0:T(32,128)(4,1)S(1)}, pred[16,12,128,128]{2,3,1,0:T(32,128)(4,1)}, u32[]{:S(2)}) copy-start(pred[16,12,128,128]{2,3,1,0:T(32,128)(4,1)} %get-tuple-element.11) | copy-start | bytes 9437188
  241.2 3.0 copy-start.12
  251.0 26.2 %copy-start.10 = (bf16[16,12,64,128]{3,2,1,0:T(8,128)(2,1)S(1)}, bf16[16,12,64,128]{3,2,1,0:T(8,128)(2,1)}, u32[]{:S(2)}) copy-start(bf16[16,12,64,128]{3,2,1,0:T(8,128)(2,1)} %copy-done.9) | copy-start | bytes 9437188
  277.2 2.5 copy-start.15
  279.6 11.4 %copy-start.14 = (bf16[16,128,768]{2,1,0:T(8,128)(2,1)S(1)}, bf16[16,128,768]{2,1,0:T(8,128)(2,1)}, u32[]{:S(2)}) copy-start(bf16[16,128,768]{2,1,0:T(8,128)(2,1)} %multiply_convert_fusion) | copy-start | bytes 9437188
  296.5 130.0 %all-reduce.6.cloned.1.call-start = ((), (), s32[]{:S(2)}) async-start(), calls=%async_computation.3 | async-start | bytes 1179648 | tf_op jit(solution)/shard_map/psum | solution.py:86
Sparse Core Ops, SparseCore 0:
  10.2 82.0 all-gather.1
  296.6 93.9 reduce-scatter.1
  393.0 33.3 all-reduce.5
where the time goes:
time: 464 us; the launch traced here: 461 us
  waiting for transfers between devices  204 us (44%)
  matrix products  83.9 us (18%)
  local copies, waits for them, and re-layouts  76.2 us (16%)
  other arithmetic  47.1 us (10%)
  blocking collectives  34.2 us (7%)
  between operations  15.2 us (3%)
    reduce_scatter x1, waiting for transfers between devices, shards(): lax.psum_scatter(jnp.concatenate([first, second], axis=1).astype(jnp.bflo...  94.1 us
    all_gather x1, waiting for transfers between devices, shards(): weights = lax.all_gather(attn_weight, 'dp', axis=0, tiled=True)  73.4 us
    psum x1, waiting for transfers between devices, shards(): shard = lax.psum(shard.astype(jnp.bfloat16), 'cand').astype(jnp.float32)  35.8 us
    add_any x1, local copies, waits for them, and re-layouts, attend(): parts[:, :, 0]  26.1 us
    dot_general x3, matrix products, attend(): jnp.einsum('bhqk,bkhd->bqhd', probs, parts[:, :, 2], preferred_element_ty...  24.4 us
    dot_general x3, matrix products, attend(): jnp.einsum('bqhd,bkhd->bhqk', parts[:, :, 0], parts[:, :, 1], preferred_e...  23.1 us
    unnamed x47, local copies, waits for them, and re-layouts  22.7 us
    psum x1, blocking collectives, shards(): squares = lax.psum(jnp.sum(shard * shard), 'dp')  22 us
  transfers between devices with their start and end apart: 3, of which 3 were waited for; matrix products, arithmetic and copies ran while one was open for 2% of the time, Pallas kernels for 0%

commit v1 on v0

--- a/solution.py
+++ b/solution.py
@@ -4,6 +4,17 @@
 from jax.sharding import PartitionSpec as P
 
 EPS = 1e-06
+
+
+def turned_line(x, axis, d):
+    size = lax.axis_size(axis)
+    right = [(i, (i + 1) % size) for i in range(size)]
+    parts = [x]
+    for hop in range(1, size):
+        parts = [lax.ppermute(parts[0], axis, right), *parts]
+    whole = jnp.concatenate(parts, axis=d)
+    shift = (lax.axis_index(axis) + 1) * parts[-1].shape[d]
+    return jnp.roll(whole, shift, axis=d)
 
 
 def rms_rows(values, gain):
@@ -38,7 +49,7 @@
 
 def shards(hidden, attn_weight, norm_gain, pos_bias, score_weight, pair_lengths, labels):
     q_local, c_local, seq, width = hidden.shape
-    weights = lax.all_gather(attn_weight, "dp", axis=0, tiled=True)
+    weights = turned_line(attn_weight, "dp", 0)
     tokens = hidden.reshape(q_local * c_local, seq, width)
     pair_len = pair_lengths.reshape(-1)
     values = tokens.astype(jnp.float32)

time: 464 us -> 501 us (1.080)
  waiting for transfers between devices: 204 us -> 227 us
  local copies, waits for them, and re-layouts: 76.2 us -> 87.5 us
    ppermute x0 -> x7, waiting for transfers between devices: none -> 98.1 us  [turned_line(): parts = [lax.ppermute(parts[0], axis, right), *parts]]
    all_gather x1 -> x0, waiting for transfers between devices: 73.4 us -> none  [shards(): weights = lax.all_gather(attn_weight, 'dp', axis=0, tiled=True)]
    unnamed x47 -> x72, local copies, waits for them, and re-layouts: 22.7 us -> 34.1 us
  transfers between devices with their start and end apart: 3 -> 9, of which waited for: 3 -> 9; matrix products, arithmetic and copies ran while one was open for 2% -> 2% of each run, Pallas kernels for 0% -> 0%
where the time goes in v1:
time: 501 us; the launch traced here: 496 us
  waiting for transfers between devices  227 us (45%)
  local copies, waits for them, and re-layouts  87.5 us (17%)
  matrix products  81.9 us (16%)
  other arithmetic  47.5 us (9%)
  blocking collectives  33.5 us (7%)
  between operations  15.6 us (3%)
    ppermute x7, waiting for transfers between devices, turned_line(): parts = [lax.ppermute(parts[0], axis, right), *parts]  98.1 us
    reduce_scatter x1, waiting for transfers between devices, shards(): lax.psum_scatter(jnp.concatenate([first, second], axis=1).astype(jnp.bflo...  93.2 us
    psum x1, waiting for transfers between devices, shards(): shard = lax.psum(shard.astype(jnp.bfloat16), 'cand').astype(jnp.float32)  35.7 us
    unnamed x72, local copies, waits for them, and re-layouts  34.1 us
    add_any x1, local copies, waits for them, and re-layouts, attend(): parts[:, :, 0]  26.1 us
    dot_general x3, matrix products, attend(): jnp.einsum('bhqk,bkhd->bqhd', probs, parts[:, :, 2], preferred_element_ty...  24.4 us
    dot_general x3, matrix products, attend(): jnp.einsum('bqhd,bkhd->bhqk', parts[:, :, 0], parts[:, :, 1], preferred_e...  23 us
    psum x1, blocking collectives, shards(): squares = lax.psum(jnp.sum(shard * shard), 'dp')  22 us
  transfers between devices with their start and end apart: 9, of which 9 were waited for; matrix products, arithmetic and copies ran while one was open for 2% of the time, Pallas kernels for 0%

profile of v1, /device:TPU:0, one launch (start us, length us, event | category | flops | bytes accessed | tf_op | source)
XLA Modules:
  0.0 496.2 jit_solution(14907487722820918671)
XLA Ops:
  7.2 3.0 collective-permute-start
  10.3 16.6 %collective-permute-done = bf16[96,3072]{1,0:T(8,128)(2,1)S(1)} collective-permute-done((bf16[96,3072]{1,0:T(8,128)(2,1)}, bf16[96,3072]{1,0:T(8,128)(2,1)S(1)}, u32[]{:S(2)}, u32[]{:S(2)}) %collective-permute-start) | collective-permute-done | bytes 589856 | tf_op jit(solution)/shard_map/ppermute | solution.py:14
  26.8 0.8 copy-done.16
  27.6 17.2 %collective-permute-done.1 = bf16[96,3072]{1,0:T(8,128)(2,1)S(1)} collective-permute-done((bf16[96,3072]{1,0:T(8,128)(2,1)S(1)}, bf16[96,3072]{1,0:T(8,128)(2,1)S(1)}, u32[]{:S(2)}, u32[]{:S(2)}) %collective-permute-start.1) | collective-permute-done | bytes 589856 | tf_op jit(solution)/shard_map/ppermute | solution.py:14
  44.8 0.8 copy-done.18
  45.7 16.4 %collective-permute-done.2 = bf16[96,3072]{1,0:T(8,128)(2,1)} collective-permute-done((bf16[96,3072]{1,0:T(8,128)(2,1)S(1)}, bf16[96,3072]{1,0:T(8,128)(2,1)}, u32[]{:S(2)}, u32[]{:S(2)}) %collective-permute-start.2) | collective-permute-done | bytes 589856 | tf_op jit(solution)/shard_map/ppermute | solution.py:14
  62.1 0.8 lt.47
  62.9 15.0 %collective-permute-done.3 = bf16[96,3072]{1,0:T(8,128)(2,1)} collective-permute-done((bf16[96,3072]{1,0:T(8,128)(2,1)}, bf16[96,3072]{1,0:T(8,128)(2,1)}, u32[]{:S(2)}, u32[]{:S(2)}) %collective-permute-start.3) | collective-permute-done | bytes 589856 | tf_op jit(solution)/shard_map/ppermute | solution.py:14
  78.0 2.3 copy.24
  80.3 2.6 multiply_reduce_fusion
  82.9 10.0 %collective-permute-done.4 = bf16[96,3072]{1,0:T(8,128)(2,1)} collective-permute-done((bf16[96,3072]{1,0:T(8,128)(2,1)}, bf16[96,3072]{1,0:T(8,128)(2,1)}, u32[]{:S(2)}, u32[]{:S(2)}) %collective-permute-start.4) | collective-permute-done | bytes 589856 | tf_op jit(solution)/shard_map/ppermute | solution.py:14
  92.9 3.1 multiply_convert_fusion.1
  96.0 10.8 %collective-permute-done.5 = bf16[96,3072]{1,0:T(8,128)(2,1)S(1)} collective-permute-done((bf16[96,3072]{1,0:T(8,128)(2,1)}, bf16[96,3072]{1,0:T(8,128)(2,1)S(1)}, u32[]{:S(2)}, u32[]{:S(2)}) %collective-permute-start.5) | collective-permute-done | bytes 589856 | tf_op jit(solution)/shard_map/ppermute | solution.py:14
  106.8 0.8 fusion.13
  107.6 12.1 %collective-permute-done.6 = bf16[96,3072]{1,0:T(8,128)(2,1)S(1)} collective-permute-done((bf16[96,3072]{1,0:T(8,128)(2,1)S(1)}, bf16[96,3072]{1,0:T(8,128)(2,1)S(1)}, u32[]{:S(2)}, u32[]{:S(2)}) %collective-permute-start.6) | collective-permute-done | bytes 589856 | tf_op jit(solution)/shard_map/ppermute | solution.py:14
  119.8 1.1 constant_dynamic-update-slice_fusion.13
  120.9 1.1 constant_dynamic-update-slice_fusion.12
  122.0 1.1 constant_dynamic-update-slice_fusion.11
  123.4 1.1 constant_dynamic-update-slice_fusion.5
  124.5 1.1 constant_dynamic-update-slice_fusion.4
  125.6 1.1 constant_dynamic-update-slice_fusion.3
  126.9 3.6 copy-done.20
  130.4 10.1 %convolution_convert_fusion = bf16[2048,2304]{1,0:T(8,128)(2,1)} fusion(bf16[2048,768]{1,0:T(8,128)(2,1)S(1)} %fusion.13, bf16[1536,3072]{1,0:T(8,128)(2,1)S(1)} %constant_dynamic-update-slice_fusion, s32[]{:T(128)S(6)} %select_n.22), kind=kOutput, calls=%fused_computation.11 | convolution fusion | flops 7252475904 | bytes 16121860 | tf_op jit(solution)/shard_map/dot_general | solution.py:58
  140.5 12.7 %copy.20 = bf16[2048,2304]{0,1:T(8,128)(2,1)} copy(bf16[2048,2304]{1,0:T(8,128)(2,1)} %convolution_convert_fusion) | data formatting | bytes 18874368 | tf_op jit(solution)/shard_map/convert_element_type | solution.py:59
  153.2 10.9 %copy.45 = bf16[288,8,16,128]{3,2,1,0:T(8,128)(2,1)} copy(bf16[288,8,16,128]{3,1,2,0:T(8,128)(2,1)} %bitcast.104) | data formatting | bytes 18874368
  164.1 6.3 %fusion.57 = (bf16[16,128,1,12,64]{1,0,4,3,2:T(8,128)(2,1)}, bf16[16,128,1,12,64]{1,0,4,3,2:T(8,128)(2,1)}, bf16[16,128,1,12,64]{1,0,4,3,2:T(8,128)(2,1)S(1)}) fusion(bf16[16,128,3,12,64]{1,0,4,3,2:T(8,128)(2,1)} %bitcast.103), kind=kLoop, calls=%fused_computation.108 | loop fusion | bytes 18874368 | tf_op jit(solution)/shard_map/jvp()/slice | solution.py:41
  170.4 7.5 %fusion.5 = (f32[16,12,128]{2,1,0:T(8,128)S(1)}, f32[16,12,128,128]{2,3,1,0:T(8,128)S(1)}) fusion(f32[12,128,128]{1,2,0:T(8,128)S(1)} %copy-done.11, pred[16,128]{1,0:T(8,128)(4,1)S(1)} %iota_compare_fusion, bf16[16,128,1,12,64]{1,0,4,3,2:T(8,128)(2,1)S(1)} %get-tuple-element.15, bf16[16,128,1,12,64]{1,0,4,3,2:T(8,128)(2,1)} %get-tuple-element.14), kind=kOutput, calls=%fused_computation.13 | convolution fusion | flops 412065792 | bytes 19761152 | tf_op jit(solution)/shard_map/jvp(bqhd,bkhd->bhqk)/dot_general | solution.py:31
  178.0 3.4 fusion.37
  181.4 1.2 copy-done
  182.6 8.1 %convert_reduce_fusion = (f32[16,12,128]{2,1,0:T(8,128)S(1)}, pred[16,12,128,128]{2,3,1,0:T(32,128)(4,1)}, bf16[16,12,128,128]{2,3,1,0:T(8,128)(2,1)S(1)}) fusion(f32[16,12,128]{2,1,0:T(8,128)S(1)} %get-tuple-element.20, f32[16,12,128,128]{2,3,1,0:T(8,128)S(1)} %get-tuple-element.21, f32[12,128,128]{1,2,0:T(8,128)S(1)} %copy-done.11, ...), kind=kLoop, calls=%fused_computation.7 | loop fusion | flops 25141248 | bytes 23103488 | tf_op jit(solution)/shard_map/jvp()/reduce_sum | solution.py:37
  190.7 2.7 fusion.36
  193.4 0.4 copy-done.2
  193.9 1.0 copy-done.6
  194.8 4.9 fusion.15
  199.9 0.2 multiply_reduce_fusion.1
  200.3 5.8 %pmax.7 = f32[2]{0:T(128)S(1)} all-reduce(f32[2]{0:T(128)S(1)} %reduce_max.19), channel_id=1, replica_groups=mesh['dp'=8,'cand'=4] {'cand'}, use_global_device_ids=true, to_apply=%region_7.8 | all-reduce | flops 2 | bytes 16 | tf_op jit(solution)/shard_map/pmax | solution.py:71
  206.1 0.2 multiply_reduce_fusion.3
  206.3 5.8 %all-reduce.3 = (f32[2]{0:T(128)S(1)}, f32[2]{0:T(128)S(1)}, f32[2]{0:T(128)S(1)}) all-reduce(f32[2]{0:T(128)S(1)} %get-tuple-element.3, f32[2]{0:T(128)S(1)} %get-tuple-element.4, f32[2]{0:T(128)S(1)} %get-tuple-element.2), channel_id=1, replica_groups=mesh['dp'=8,'cand'=4] {'cand'}, use_global_device_ids=true, to_apply=%region_11.12 | all-reduce | flops 6 | bytes 48 | tf_op jit(solution)/shard_map/psum | solution.py:72
  212.2 0.2 fusion.45
  212.5 0.4 fusion.11
  213.0 5.5 %convolution_convert_fusion.2 = bf16[2048,768]{1,0:T(8,128)(2,1)} fusion(bf16[2048,768]{1,0:T(8,128)(2,1)S(1)} %fusion.11, bf16[1536,3072]{1,0:T(8,128)(2,1)} %copy-done.20, s32[]{:T(128)S(6)} %select_n.22, s32[]{:T(128)S(6)} %add.82), kind=kOutput, calls=%fused_computation.41 | convolution fusion | flops 2417491968 | bytes 7471112 | tf_op jit(solution)/shard_map/dot_general | solution.py:85
  218.5 4.7 copy.27
  223.2 2.9 copy.46
  226.1 1.6 copy-done.12
  227.7 9.0 %convert_bitcast_fusion.2 = bf16[16,128,1,12,64]{1,4,3,0,2:T(8,128)(2,1)} fusion(bf16[16,12,128,128]{2,3,1,0:T(8,128)(2,1)} %copy-done.2, bf16[16,12,64,128]{3,0,2,1:T(8,128)(2,1)S(1)} %bitcast.108), kind=kOutput, calls=%fused_computation.50 | convolution fusion | flops 404226048 | bytes 12582912 | tf_op jit(solution)/shard_map/transpose(jvp(bhqk,bkhd->bqhd))/dot_general | solution.py:40
  236.8 12.6 %fusion.3 = (f32[16,12,128]{2,1,0:T(8,128)S(1)}, bf16[16,12,128,128]{2,3,1,0:T(8,128)(2,1)}) fusion(f32[16,12,128]{2,1,0:T(8,128)S(1)} %multiply_divide_fusion, f32[16,12,128]{2,1,0:T(8,128)S(1)} %get-tuple-element.20, f32[16,12,128,128]{2,3,1,0:T(8,128)} %copy-done, f32[12,128,128]{1,2,0:T(8,128)S(1)} %copy-done.11, ...), kind=kOutput, calls=%fused_computation.5 | convolution fusion | flops 427794432 | bytes 26249216 | tf_op jit(solution)/shard_map/transpose(jvp(bhqk,bkhd->bqhd))/dot_general | solution.py:40
  249.5 10.1 %fusion.54 = (f32[16,12,128]{2,1,0:T(8,128)S(1)}, f32[16,12,128,128]{2,3,1,0:T(8,128)}) fusion(f32[16,12,128]{2,1,0:T(8,128)S(1)} %get-tuple-element.20, f32[16,12,128,128]{2,3,1,0:T(8,128)S(1)} %bitcast.102, f32[12,128,128]{1,2,0:T(8,128)S(1)} %copy-done.11, pred[16,128]{1,0:T(8,128)(4,1)S(1)} %iota_compare_fusion, f32[16,12,128]{2,1,0:T(8,128)S(1)} %neg.9, ...), kind=kLoop, calls=%fused_computation.107 | loop fusion | flops 25141248 | bytes 32638976 | tf_op jit(solution)/shard_map/transpose(jvp())/reduce_sum | solution.py:38
  259.7 11.3 %convert_bitcast_fusion.1 = bf16[16,128,1,12,64]{1,4,3,0,2:T(8,128)(2,1)} fusion(bf16[16,128,1,12,64]{1,0,4,3,2:T(8,128)(2,1)} %get-tuple-element.14, f32[16,12,128,128]{2,3,1,0:T(8,128)} %get-tuple-element.9, pred[16,12,128,128]{2,3,1,0:T(32,128)(4,1)} %get-tuple-element.11, f32[16,12,128]{2,1,0:T(8,128)S(1)} %negate_divide_fusion, ...), kind=kOutput, calls=%fused_computation.49 | convolution fusion | flops 413663232 | bytes 22120448 | tf_op jit(solution)/shard_map/transpose(jvp(bqhd,bkhd->bhqk))/dot_general | solution.py:31
  270.9 0.7 copy-done.4
  271.6 0.9 copy-done.7
  272.5 4.2 convert_bitcast_fusion
  276.7 2.1 multiply_convert_fusion
  278.9 8.2 %pad_add_fusion = bf16[16,128,3,12,64]{1,4,3,0,2:T(8,128)(2,1)} fusion(bf16[16,128,1,12,64]{1,4,3,0,2:T(8,128)(2,1)} %convert_bitcast_fusion, bf16[16,128,1,12,64]{1,4,3,0,2:T(8,128)(2,1)} %convert_bitcast_fusion.1, bf16[16,128,1,12,64]{1,4,3,0,2:T(8,128)(2,1)} %convert_bitcast_fusion.2), kind=kLoop, calls=%fused_computation.17 | loop fusion | flops 9437184 | bytes 18874368 | tf_op jit(solution)/shard_map/transpose(jvp())/add_any | solution.py:32
  287.1 26.1 %copy.33 = bf16[16,128,3,12,64]{1,0,4,3,2:T(8,128)(2,1)} copy(bf16[16,128,3,12,64]{1,4,3,0,2:T(8,128)(2,1)} %pad_add_fusion) | data formatting | bytes 18874368 | tf_op jit(solution)/shard_map/transpose(jvp())/add_any | solution.py:32
  313.2 2.4 copy.34
  315.7 11.4 %fusion.22 = bf16[768,2304]{1,0:T(8,128)(2,1)S(1)} fusion(bf16[2048,768]{1,0:T(8,128)(2,1)S(1)} %bitcast.113, bf16[288,8,16,128]{3,2,1,0:T(8,128)(2,1)} %bitcast.110), kind=kOutput, calls=%fused_computation.37 | convolution fusion | flops 7249526784 | bytes 16121856 | tf_op jit(solution)/shard_map/dot_general | solution.py:89
  327.1 2.6 fusion.38
  329.7 2.8 pad_maximum_fusion
  332.6 93.2 %reduce-scatter.2.cloned.1.call-done = bf16[96,3072]{1,0:T(8,128)(2,1)} async-done(((bf16[768,3072]{1,0:T(8,128)(2,1)}), bf16[96,3072]{1,0:T(8,128)(2,1)}) %reduce-scatter.2.cloned.1.call-update) | async-done | bytes 589840 | tf_op jit(solution)/shard_map/reduce_scatter | solution.py:91
  425.8 35.7 %all-reduce.6.cloned.1.call-done = bf16[96,3072]{1,0:T(8,128)(2,1)} async-done(((bf16[96,3072]{1,0:T(8,128)(2,1)}), bf16[96,3072]{1,0:T(8,128)(2,1)}) %all-reduce.6.cloned.1.call-update) | async-done | bytes 589840 | tf_op jit(solution)/shard_map/psum | solution.py:97
  461.6 2.0 fusion.41
  463.5 0.5 divide_subtract_fusion.1
  464.0 22.0 %psum.38 = f32[]{:T(128)} all-reduce(f32[]{:T(128)} %fusion.41), channel_id=1, replica_groups=mesh['dp'=8,'cand'=4] {'dp'}, use_global_device_ids=true, to_apply=%region_19.20 | all-reduce | flops 1 | bytes 8 | tf_op jit(solution)/shard_map/psum | solution.py:98
  486.7 2.2 convert_divide_fusion.1
  (81 shorter events, 1.4 us)
Async XLA Ops:
  7.2 85.8 %copy-start.5 = (bf16[2,8,128,768]{3,2,1,0:T(8,128)(2,1)S(1)}, bf16[2,8,128,768]{3,2,1,0:T(8,128)(2,1)}, u32[]{:S(2)}) copy-start(bf16[2,8,128,768]{3,2,1,0:T(8,128)(2,1)} %param.7) | copy-start | bytes 9437188
  7.2 99.6 %copy-start.22 = (f32[768]{0:T(1024)S(1)}, f32[768]{0:T(1024)}, u32[]{:S(2)}) copy-start(f32[768]{0:T(1024)} %param.9) | copy-start | bytes 9220
  7.2 418.6 %reduce-scatter.2.cloned.1.call-start = ((), (), s32[]{:S(2)}) async-start(), calls=%async_computation.1 | async-start | bytes 5308416 | tf_op jit(solution)/shard_map/reduce_scatter | solution.py:91
  7.2 19.6 %collective-permute-start = (bf16[96,3072]{1,0:T(8,128)(2,1)}, bf16[96,3072]{1,0:T(8,128)(2,1)S(1)}, u32[]{:S(2)}, u32[]{:S(2)}) collective-permute-start(bf16[96,3072]{1,0:T(8,128)(2,1)} %param.8), channel_id=1, source_target_pairs={{0,4},{4,8},{8,12},{12,16},{16,20},{20,24},{24,28},{28,0},{1,5},{5... | collective-permute-start | bytes 1769480 | tf_op jit(solution)/shard_map/ppermute | solution.py:14
  26.8 0.8 copy-start.16
  27.6 17.2 %collective-permute-start.1 = (bf16[96,3072]{1,0:T(8,128)(2,1)S(1)}, bf16[96,3072]{1,0:T(8,128)(2,1)S(1)}, u32[]{:S(2)}, u32[]{:S(2)}) collective-permute-start(bf16[96,3072]{1,0:T(8,128)(2,1)S(1)} %collective-permute-done), channel_id=1, source_target_pairs={{0,4},{4,8},{8,12},{12,16},{16,20},{20,24},{24,28},{28,0},{1,5},{5... | collective-permute-start | bytes 1769480 | tf_op jit(solution)/shard_map/ppermute | solution.py:14
  44.8 0.8 copy-start.18
  45.7 16.4 %collective-permute-start.2 = (bf16[96,3072]{1,0:T(8,128)(2,1)S(1)}, bf16[96,3072]{1,0:T(8,128)(2,1)}, u32[]{:S(2)}, u32[]{:S(2)}) collective-permute-start(bf16[96,3072]{1,0:T(8,128)(2,1)S(1)} %collective-permute-done.1), channel_id=1, source_target_pairs={{0,4},{4,8},{8,12},{12,16},{16,20},{20,24},{24,28},{28,0},{1,5},{5... | collective-permute-start | bytes 1769480 | tf_op jit(solution)/shard_map/ppermute | solution.py:14
  62.1 15.8 %collective-permute-start.3 = (bf16[96,3072]{1,0:T(8,128)(2,1)}, bf16[96,3072]{1,0:T(8,128)(2,1)}, u32[]{:S(2)}, u32[]{:S(2)}) collective-permute-start(bf16[96,3072]{1,0:T(8,128)(2,1)} %collective-permute-done.2), channel_id=1, source_target_pairs={{0,4},{4,8},{8,12},{12,16},{16,20},{20,24},{24,28},{28,0},{1,5},{5... | collective-permute-start | bytes 1769480 | tf_op jit(solution)/shard_map/ppermute | solution.py:14
  77.9 14.9 %collective-permute-start.4 = (bf16[96,3072]{1,0:T(8,128)(2,1)}, bf16[96,3072]{1,0:T(8,128)(2,1)}, u32[]{:S(2)}, u32[]{:S(2)}) collective-permute-start(bf16[96,3072]{1,0:T(8,128)(2,1)} %collective-permute-done.3), channel_id=1, source_target_pairs={{0,4},{4,8},{8,12},{12,16},{16,20},{20,24},{24,28},{28,0},{1,5},{5... | collective-permute-start | bytes 1769480 | tf_op jit(solution)/shard_map/ppermute | solution.py:14
  92.8 14.0 %collective-permute-start.5 = (bf16[96,3072]{1,0:T(8,128)(2,1)}, bf16[96,3072]{1,0:T(8,128)(2,1)S(1)}, u32[]{:S(2)}, u32[]{:S(2)}) collective-permute-start(bf16[96,3072]{1,0:T(8,128)(2,1)} %collective-permute-done.4), channel_id=1, source_target_pairs={{0,4},{4,8},{8,12},{12,16},{16,20},{20,24},{24,28},{28,0},{1,5},{5... | collective-permute-start | bytes 1769480 | tf_op jit(solution)/shard_map/ppermute | solution.py:14
  96.0 27.1 %copy-start.19 = (bf16[96,3072]{1,0:T(8,128)(2,1)S(1)}, bf16[96,3072]{1,0:T(8,128)(2,1)}, u32[]{:S(2)}) copy-start(bf16[96,3072]{1,0:T(8,128)(2,1)} %copy-done.18) | copy-start | bytes 1769476
  106.8 12.9 %collective-permute-start.6 = (bf16[96,3072]{1,0:T(8,128)(2,1)S(1)}, bf16[96,3072]{1,0:T(8,128)(2,1)S(1)}, u32[]{:S(2)}, u32[]{:S(2)}) collective-permute-start(bf16[96,3072]{1,0:T(8,128)(2,1)S(1)} %collective-permute-done.5), channel_id=1, source_target_pairs={{0,4},{4,8},{8,12},{12,16},{16,20},{20,24},{24,28},{28,0},{1,5},{5... | collective-permute-start | bytes 1769480 | tf_op jit(solution)/shard_map/ppermute | solution.py:14
  106.8 16.4 %copy-start.17 = (bf16[96,3072]{1,0:T(8,128)(2,1)S(1)}, bf16[96,3072]{1,0:T(8,128)(2,1)}, u32[]{:S(2)}) copy-start(bf16[96,3072]{1,0:T(8,128)(2,1)} %copy-done.16) | copy-start | bytes 1769476
  106.8 16.4 %copy-start.15 = (bf16[96,3072]{1,0:T(8,128)(2,1)S(1)}, bf16[96,3072]{1,0:T(8,128)(2,1)}, u32[]{:S(2)}) copy-start(bf16[96,3072]{1,0:T(8,128)(2,1)} %param.8) | copy-start | bytes 1769476
  126.9 3.6 copy-start.20
  164.1 6.3 %copy-start.11 = (f32[12,128,128]{1,2,0:T(8,128)S(1)}, f32[12,128,128]{1,2,0:T(8,128)}, u32[]{:S(2)}) copy-start(f32[12,128,128]{1,2,0:T(8,128)} %copy.24) | copy-start | bytes 2359300
  170.4 7.6 %copy-start.3 = (bf16[16,128,1,12,64]{1,0,4,3,2:T(8,128)(2,1)}, bf16[16,128,1,12,64]{1,0,4,3,2:T(8,128)(2,1)S(1)}, u32[]{:S(2)}) copy-start(bf16[16,128,1,12,64]{1,0,4,3,2:T(8,128)(2,1)S(1)} %get-tuple-element.15) | copy-start | bytes 9437188
  178.0 4.6 copy-start
  182.6 8.1 %copy-start.8 = (bf16[16,128,1,12,64]{1,0,4,3,2:T(8,128)(2,1)S(1)}, bf16[16,128,1,12,64]{1,0,4,3,2:T(8,128)(2,1)}, u32[]{:S(2)}) copy-start(bf16[16,128,1,12,64]{1,0,4,3,2:T(8,128)(2,1)} %get-tuple-element.13) | copy-start | bytes 9437188
  190.7 3.2 copy-start.2
  190.7 4.2 copy-start.6
  193.9 5.9 %copy-start.9 = (bf16[16,12,64,128]{3,2,1,0:T(8,128)(2,1)}, bf16[16,12,64,128]{3,2,1,0:T(8,128)(2,1)S(1)}, u32[]{:S(2)}) copy-start(bf16[16,12,64,128]{3,2,1,0:T(8,128)(2,1)S(1)} %fusion.36) | copy-start | bytes 9437188
  194.8 5.1 %copy-start.21 = (f32[768]{0:T(1024)S(1)}, f32[768]{0:T(1024)}, u32[]{:S(2)}) copy-start(f32[768]{0:T(1024)} %param.11) | copy-start | bytes 9220
  194.8 11.3 %copy-start.23 = (s32[2,8]{1,0:T(2,128)S(1)}, s32[2,8]{1,0:T(2,128)}, u32[]{:S(2)}) copy-start(s32[2,8]{1,0:T(2,128)} %param.13) | copy-start | bytes 196
  226.1 1.6 copy-start.12
  227.7 21.7 %slice-start = ((s8[12582912]{0:T(1024)(128)(4,1)}), s8[4194304]{0:T(1024)(128)(4,1)S(1)}, s32[]{:S(2)}) async-start(s8[12582912]{0:T(1024)(128)(4,1)} %bitcast.101), calls=%async_computation.3 | async-start | bytes 8388608
  236.8 12.7 %slice-start.1 = ((s8[12582912]{0:T(1024)(128)(4,1)}), s8[4194304]{0:T(1024)(128)(4,1)S(1)}, s32[]{:S(2)}) async-start(s8[12582912]{0:T(1024)(128)(4,1)} %bitcast.101), calls=%async_computation.4 | async-start | bytes 8388608
  236.8 12.7 %slice-start.2 = ((s8[12582912]{0:T(1024)(128)(4,1)}), s8[4194304]{0:T(1024)(128)(4,1)S(1)}, s32[]{:S(2)}) async-start(s8[12582912]{0:T(1024)(128)(4,1)} %bitcast.101), calls=%async_computation.5 | async-start | bytes 8388608
  259.6 11.3 %copy-start.1 = (f32[16,12,128,128]{2,3,1,0:T(8,128)S(1)}, f32[16,12,128,128]{2,3,1,0:T(8,128)}, u32[]{:S(2)}) copy-start(f32[16,12,128,128]{2,3,1,0:T(8,128)} %get-tuple-element.9) | copy-start | bytes 37748740
  259.7 12.0 %copy-start.4 = (bf16[16,128,1,12,64]{1,0,4,3,2:T(8,128)(2,1)S(1)}, bf16[16,128,1,12,64]{1,0,4,3,2:T(8,128)(2,1)}, u32[]{:S(2)}) copy-start(bf16[16,128,1,12,64]{1,0,4,3,2:T(8,128)(2,1)} %copy-done.3) | copy-start | bytes 9437188
  259.7 12.9 %copy-start.7 = (pred[16,12,128,128]{2,3,1,0:T(32,128)(4,1)S(1)}, pred[16,12,128,128]{2,3,1,0:T(32,128)(4,1)}, u32[]{:S(2)}) copy-start(pred[16,12,128,128]{2,3,1,0:T(32,128)(4,1)} %get-tuple-element.11) | copy-start | bytes 9437188
  287.1 26.2 %copy-start.10 = (bf16[16,12,64,128]{3,2,1,0:T(8,128)(2,1)S(1)}, bf16[16,12,64,128]{3,2,1,0:T(8,128)(2,1)}, u32[]{:S(2)}) copy-start(bf16[16,12,64,128]{3,2,1,0:T(8,128)(2,1)} %copy-done.9) | copy-start | bytes 9437188
  313.2 2.5 copy-start.14
  315.7 11.4 %copy-start.13 = (bf16[16,128,768]{2,1,0:T(8,128)(2,1)S(1)}, bf16[16,128,768]{2,1,0:T(8,128)(2,1)}, u32[]{:S(2)}) copy-start(bf16[16,128,768]{2,1,0:T(8,128)(2,1)} %multiply_convert_fusion) | copy-start | bytes 9437188
  332.5 129.0 %all-reduce.6.cloned.1.call-start = ((), (), s32[]{:S(2)}) async-start(), calls=%async_computation.2 | async-start | bytes 1179648 | tf_op jit(solution)/shard_map/psum | solution.py:97
Sparse Core Ops, SparseCore 0:
  332.6 93.1 reduce-scatter.1
  428.1 33.3 all-reduce.5
